TPU v7x, 32 devices: a whole 2x2x4 slice. The times are simulated.
32 devices in a mesh: row: 4 (over z), col: 4 (over y, x), layer: 2 (over core).
Axes of the slice: x: 2, y: 2, z: 4, core: 2. Of those that a mesh axis runs over, the one named last changes fastest.
Arguments:
- wavefunction: float32 [4096, 4096], P('row', 'col'), may hold values from -0.015625 to 1.515625
- start_block: float32 [4096, 2048], P(('col', 'layer'), 'row'), may hold values from -6 to 6
Outputs:
- basis: float32 [4096, 2048], P(('col', 'layer'), 'row')
All inputs are finite; a program needn't handle non-finite values.
Results may differ from a plain program's by a relative error of at most 0.0003.
Values sent between devices are 32-bit elements; how exact they have to be, the bound alone decides.
No kernel may reach another device: no remote copies, remote signals or barrier semaphores. Data moves between devices by JAX's collectives and lax.ppermute only.
A program may use at most 128 MiB of HBM per device.

v0:
```python
import math
import jax
import jax.numpy as jnp
from jax import lax
from jax.sharding import PartitionSpec as P


def spread(x, axis, root):
    mine = lax.axis_index(axis) == root
    return lax.psum(jnp.where(mine, x, jnp.zeros_like(x)), axis)


def cross(left, right):
    return lax.dot_general(
        left,
        right,
        (((0,), (0,)), ((), ())),
        precision=lax.Precision.HIGHEST,
        preferred_element_type=jnp.float32,
    )


def times(left, right):
    return jnp.dot(left, right, precision=lax.Precision.HIGHEST, preferred_element_type=jnp.float32)


def apply_density(rho_slab, basis_block):
    return lax.psum_scatter(
        cross(rho_slab, basis_block), ("col", "layer"), scatter_dimension=0, tiled=True
    )


def orthonormalize(image_block):
    panel_owner = lax.axis_index("row")
    panels = lax.axis_size("row")
    current = image_block
    gram_matrix = lax.psum(cross(current, current), ("col", "layer"))
    for panel_index in range(panels):
        factor = jnp.linalg.cholesky(gram_matrix)
        new_basis = jax.scipy.linalg.solve_triangular(factor, current.T, lower=True).T
        current = jnp.where(panel_owner == panel_index, new_basis, current)
        if panel_index + 1 < panels:
            chosen = spread(current, "row", panel_index)
            later = panel_owner > panel_index
            correlation, square = lax.psum(
                (cross(chosen, current), cross(current, current)), ("col", "layer")
            )
            current = jnp.where(later, current - times(chosen, correlation), current)
            gram_matrix = jnp.where(later, square - cross(correlation, correlation), square)
    return current


def shards(wavefunction, start_block):
    layers = lax.axis_size("layer")
    column_width = wavefunction.shape[1] // layers
    own_slice = lax.dynamic_slice_in_dim(
        wavefunction, lax.axis_index("layer") * column_width, column_width, 1
    )
    own_rows = lax.all_gather(own_slice, "col", axis=1, tiled=True)
    partner = spread(own_rows, "row", lax.axis_index("col"))
    rho_part = lax.psum_scatter(
        lax.dot_general(
            partner,
            own_rows,
            (((1,), (1,)), ((), ())),
            precision=lax.Precision.HIGHEST,
            preferred_element_type=jnp.float32,
        ),
        "layer",
        scatter_dimension=0,
        tiled=True,
    )
    rho_slab = lax.all_gather(rho_part, "row", axis=1, tiled=True)
    current = start_block
    image_block = apply_density(rho_slab, current)
    current = orthonormalize(image_block)
    return current * math.sqrt(rho_slab.shape[1])


def solution(mesh):
    placed = (P("row", "col"), P(("col", "layer"), "row"))
    return jax.shard_map(
        shards, mesh=mesh, in_specs=placed, out_specs=P(("col", "layer"), "row"), check_vma=False
    )
```

profile of v0, /device:TPU:0, one launch (start us, length us, event | category | flops | bytes accessed | tf_op | source)
XLA Modules:
  0.0 1721.6 jit_solution(5460350467099761118)
XLA Ops:
  9.9 90.3 %all-gather.3.cloned.1.call-done = f32[1024,2048]{1,0:T(8,128)} async-done(((f32[1024,512]{1,0:T(8,128)}), f32[1024,2048]{1,0:T(8,128)}) %all-gather.3.cloned.1.call-update) | async-done | bytes 8388624 | tf_op jit(solution)/shard_map/all_gather | solution.py:59
  108.5 290.9 %all-reduce.13.cloned.1.call-done = f32[1024,2048]{1,0:T(8,128)} async-done(((f32[1024,2048]{1,0:T(8,128)}), f32[1024,2048]{1,0:T(8,128)}) %all-reduce.13.cloned.1.call-update) | async-done | bytes 8388624 | tf_op jit(solution)/shard_map/psum | solution.py:10
  399.4 32.1 %fusion.156 = f32[1024,1024]{1,0:T(8,128)} fusion(f32[1024,2048]{1,0:T(8,128)} %all-reduce.13.cloned.1.call-done, f32[1024,2048]{1,0:T(8,128)} %all-gather.3.cloned.1.call-done), kind=kOutput, calls=%fused_computation.284 | convolution fusion | flops 25769803776 | bytes 20971520 | tf_op jit(solution)/shard_map/dot_general | solution.py:62
  431.6 11.1 reduce-scatter.3.cloned.1.call-done
  443.1 152.0 %all-gather.5.cloned.1.call-done = f32[512,4096]{1,0:T(8,128)} async-done(((f32[512,1024]{1,0:T(8,128)}), f32[512,4096]{1,0:T(8,128)}) %all-gather.5.cloned.1.call-update) | async-done | bytes 8388624 | tf_op jit(solution)/shard_map/all_gather | solution.py:73
  595.1 17.1 fusion.157
  612.2 69.6 %reduce-scatter.5.cloned.1.call-done = f32[512,512]{0,1:T(8,128)} async-done(((f32[4096,512]{0,1:T(8,128)}), f32[512,512]{0,1:T(8,128)}) %reduce-scatter.5.cloned.1.call-update) | async-done | bytes 1048592 | tf_op jit(solution)/shard_map/reduce_scatter | solution.py:28
  686.9 56.3 %all-reduce.15.cloned.1.call-done = f32[512,512]{0,1:T(8,128)} async-done(((f32[512,512]{0,1:T(8,128)}), f32[512,512]{0,1:T(8,128)}) %all-reduce.15.cloned.1.call-update) | async-done | bytes 1048592 | tf_op jit(solution)/shard_map/psum | solution.py:37
  746.2 11.7 cholesky.462
  757.9 9.8 custom-call.35
  768.6 11.7 cholesky.481
  780.3 10.0 custom-call.36
  790.9 11.7 cholesky.502
  803.4 9.8 custom-call.37
  813.8 11.7 cholesky.519
  838.3 39.3 %custom-call.38 = f32[4,128,128]{1,2,0:T(8,128)S(1)} custom-call(f32[4,128,128]{2,1,0:T(8,128)S(1)} %get-tuple-element.33), custom_call_target="InvertDiagBlocksLowerTriangular" | custom-call | tf_op jit(solution)/shard_map/jit(_solve_triangular)/triangular_solve | solution.py:40
  884.9 48.4 %all-reduce.17.cloned.1.call-done = f32[512,512]{0,1:T(8,128)} async-done(((f32[512,512]{0,1:T(8,128)}), f32[512,512]{0,1:T(8,128)}) %all-reduce.17.cloned.1.call-update) | async-done | bytes 1048592 | tf_op jit(solution)/shard_map/psum | solution.py:10
  937.8 60.8 %all-reduce.27.cloned.1.call-done = (f32[512,512]{1,0:T(8,128)}, f32[512,512]{0,1:T(8,128)}) async-done(((f32[512,512]{1,0:T(8,128)}, f32[512,512]{0,1:T(8,128)}), (f32[512,512]{1,0:T(8,128)}, f32[512,512]{0,1:T(8,128)})) %all-reduce.27.cloned.1.call-update) | async-done | bytes 2097168 | tf_op jit(solution)/shard_map/psum | solution.py:45
  1006.3 11.7 cholesky.534
  1018.2 9.8 custom-call.39
  1030.6 11.9 cholesky.553
  1043.8 9.8 custom-call.40
  1055.2 11.7 cholesky.574
  1067.6 9.8 custom-call.41
  1078.8 12.1 cholesky.591
  1095.2 11.4 while.9
  1106.6 39.3 %custom-call.42 = f32[4,128,128]{1,2,0:T(8,128)S(1)} custom-call(f32[4,128,128]{2,1,0:T(8,128)S(1)} %get-tuple-element.34), custom_call_target="InvertDiagBlocksLowerTriangular" | custom-call | tf_op jit(solution)/shard_map/jit(_solve_triangular)/triangular_solve | solution.py:40
  1159.0 48.2 %all-reduce.19.cloned.1.call-done = f32[512,512]{0,1:T(8,128)} async-done(((f32[512,512]{0,1:T(8,128)}), f32[512,512]{0,1:T(8,128)}) %all-reduce.19.cloned.1.call-update) | async-done | bytes 1048592 | tf_op jit(solution)/shard_map/psum | solution.py:10
  1211.5 61.1 %all-reduce.25.cloned.1.call-done = (f32[512,512]{1,0:T(8,128)}, f32[512,512]{0,1:T(8,128)}) async-done(((f32[512,512]{1,0:T(8,128)}, f32[512,512]{0,1:T(8,128)}), (f32[512,512]{1,0:T(8,128)}, f32[512,512]{0,1:T(8,128)})) %all-reduce.25.cloned.1.call-update) | async-done | bytes 2097168 | tf_op jit(solution)/shard_map/psum | solution.py:45
  1280.2 11.7 cholesky.606
  1292.1 9.8 custom-call.43
  1304.5 11.9 cholesky.625
  1317.7 9.8 custom-call.44
  1329.1 11.7 cholesky.646
  1341.5 9.8 custom-call.45
  1352.8 12.1 cholesky.663
  1369.2 11.4 while.10
  1380.5 39.3 %custom-call.46 = f32[4,128,128]{1,2,0:T(8,128)S(1)} custom-call(f32[4,128,128]{2,1,0:T(8,128)S(1)} %get-tuple-element.35), custom_call_target="InvertDiagBlocksLowerTriangular" | custom-call | tf_op jit(solution)/shard_map/jit(_solve_triangular)/triangular_solve | solution.py:40
  1433.1 48.0 %all-reduce.21.cloned.1.call-done = f32[512,512]{0,1:T(8,128)} async-done(((f32[512,512]{0,1:T(8,128)}), f32[512,512]{0,1:T(8,128)}) %all-reduce.21.cloned.1.call-update) | async-done | bytes 1048592 | tf_op jit(solution)/shard_map/psum | solution.py:10
  1485.2 61.3 %all-reduce.23.cloned.1.call-done = (f32[512,512]{1,0:T(8,128)}, f32[512,512]{0,1:T(8,128)}) async-done(((f32[512,512]{1,0:T(8,128)}, f32[512,512]{0,1:T(8,128)}), (f32[512,512]{1,0:T(8,128)}, f32[512,512]{0,1:T(8,128)})) %all-reduce.23.cloned.1.call-update) | async-done | bytes 2097168 | tf_op jit(solution)/shard_map/psum | solution.py:45
  1554.2 11.7 cholesky.678
  1567.0 10.0 custom-call.47
  1580.2 11.7 cholesky.697
  1606.0 11.7 cholesky.718
  1619.1 10.2 custom-call.49
  1631.5 11.7 cholesky.735
  1650.2 13.7 while.11
  1663.9 40.1 %custom-call.50 = f32[4,128,128]{1,2,0:T(8,128)S(1)} custom-call(f32[4,128,128]{2,1,0:T(8,128)} %get-tuple-element.36), custom_call_target="InvertDiagBlocksLowerTriangular" | custom-call | tf_op jit(solution)/shard_map/jit(_solve_triangular)/triangular_solve | solution.py:40
  (229 shorter events, 202.7 us)
Async XLA Ops:
  6.5 588.5 %copy-start = (f32[512,512]{1,0:T(8,128)S(1)}, f32[512,512]{1,0:T(8,128)}, u32[]{:S(2)}) copy-start(f32[512,512]{1,0:T(8,128)} %param.6) | copy-start | bytes 3145732
  6.5 93.6 %all-gather.3.cloned.1.call-start = ((), (), s32[]{:S(2)}) async-start(), calls=%async_computation.2 | async-start | bytes 10485760 | tf_op jit(solution)/shard_map/all_gather | solution.py:59
  9.8 389.6 %all-reduce.13.cloned.1.call-start = ((), (), s32[]{:S(2)}) async-start(), calls=%async_computation.3 | async-start | bytes 16777216 | tf_op jit(solution)/shard_map/psum | solution.py:10
  108.4 334.3 %reduce-scatter.3.cloned.1.call-start = ((), (), s32[]{:S(2)}) async-start(), calls=%async_computation.4 | async-start | bytes 6291456 | tf_op jit(solution)/shard_map/reduce_scatter | solution.py:61
  431.5 163.5 %all-gather.5.cloned.1.call-start = ((), (), s32[]{:S(2)}) async-start(), calls=%async_computation.5 | async-start | bytes 10485760 | tf_op jit(solution)/shard_map/all_gather | solution.py:73
  442.7 239.1 %reduce-scatter.5.cloned.1.call-start = ((), (), s32[]{:S(2)}) async-start(), calls=%async_computation.6 | async-start | bytes 9437184 | tf_op jit(solution)/shard_map/reduce_scatter | solution.py:28
  612.2 131.0 %all-reduce.15.cloned.1.call-start = ((), (), s32[]{:S(2)}) async-start(), calls=%async_computation.7 | async-start | bytes 2097152 | tf_op jit(solution)/shard_map/psum | solution.py:37
  681.8 195.8 %copy-start.2 = (f32[512,512]{0,1:T(8,128)S(1)}, f32[512,512]{0,1:T(8,128)}, u32[]{:S(2)}) copy-start(f32[512,512]{0,1:T(8,128)} %reduce-scatter.5.cloned.1.call-done) | copy-start | bytes 3145732
  686.3 247.0 %all-reduce.17.cloned.1.call-start = ((), (), s32[]{:S(2)}) async-start(), calls=%async_computation.8 | async-start | bytes 2097152 | tf_op jit(solution)/shard_map/psum | solution.py:10
  882.0 116.7 %all-reduce.27.cloned.1.call-start = ((), (), s32[]{:S(2)}) async-start(), calls=%async_computation.13 | async-start | bytes 4194304 | tf_op jit(solution)/shard_map/psum | solution.py:45
  937.4 269.8 %all-reduce.19.cloned.1.call-start = ((), (), s32[]{:S(2)}) async-start(), calls=%async_computation.9 | async-start | bytes 2097152 | tf_op jit(solution)/shard_map/psum | solution.py:10
  998.7 147.3 %copy-start.4 = (f32[512,512]{1,0:T(8,128)S(1)}, f32[512,512]{1,0:T(8,128)}, u32[]{:S(2)}) copy-start(f32[512,512]{1,0:T(8,128)} %get-tuple-element.73) | copy-start | bytes 3145732
  1005.4 1.0 copy-start.6
  1156.1 116.5 %all-reduce.25.cloned.1.call-start = ((), (), s32[]{:S(2)}) async-start(), calls=%async_computation.12 | async-start | bytes 4194304 | tf_op jit(solution)/shard_map/psum | solution.py:45
  1211.3 269.9 %all-reduce.21.cloned.1.call-start = ((), (), s32[]{:S(2)}) async-start(), calls=%async_computation.10 | async-start | bytes 2097152 | tf_op jit(solution)/shard_map/psum | solution.py:10
  1272.6 147.3 %copy-start.5 = (f32[512,512]{1,0:T(8,128)S(1)}, f32[512,512]{1,0:T(8,128)}, u32[]{:S(2)}) copy-start(f32[512,512]{1,0:T(8,128)} %get-tuple-element.71) | copy-start | bytes 3145732
  1279.3 1.0 copy-start.7
  1430.1 116.5 %all-reduce.23.cloned.1.call-start = ((), (), s32[]{:S(2)}) async-start(), calls=%async_computation.11 | async-start | bytes 4194304 | tf_op jit(solution)/shard_map/psum | solution.py:45
  1546.5 157.5 %copy-start.3 = (f32[512,512]{1,0:T(8,128)S(1)}, f32[512,512]{1,0:T(8,128)}, u32[]{:S(2)}) copy-start(f32[512,512]{1,0:T(8,128)} %get-tuple-element.69) | copy-start | bytes 3145732
  1553.2 1.0 copy-start.8
  1647.0 67.5 %copy-start.1 = (f32[512,512]{1,0:T(8,128)S(1)}, f32[512,512]{1,0:T(8,128)}, u32[]{:S(2)}) copy-start(f32[512,512]{1,0:T(8,128)} %param.6) | copy-start | bytes 3145732
Sparse Core Ops, SparseCore 0:
  9.9 90.1 all-gather.2
  108.5 290.8 all-reduce.12
  431.7 10.9 reduce-scatter.2
  444.1 150.8 all-gather.4
  612.3 69.4 reduce-scatter.4
  686.4 56.6 all-reduce.14
  882.1 51.1 all-reduce.16
  937.5 61.1 all-reduce.26
  1156.2 50.9 all-reduce.18
  1211.4 61.1 all-reduce.24
  1430.2 50.9 all-reduce.20
  1485.3 61.1 all-reduce.22
where the time goes:
time: 1730 us; the launch traced here: 1720 us
  waiting for transfers between devices  998 us (58%)
  other arithmetic  500 us (29%)
  matrix products  136 us (8%)
  local copies, waits for them, and re-layouts  59.8 us (3%)
  between operations  24.6 us (1%)
    psum x4, waiting for transfers between devices, spread(): return lax.psum(jnp.where(mine, x, jnp.zeros_like(x)), axis)  436 us
    another operation x59, other arithmetic, orthonormalize(): factor = jnp.linalg.cholesky(gram_matrix)  319 us
    psum x3, waiting for transfers between devices, orthonormalize(): lax.psum((cross(chosen, current), cross(current, current)), ('col', 'laye...  183 us
    another operation x9, other arithmetic, orthonormalize(): jax.scipy.linalg.solve_triangular(factor, current.T, lower=True)  163 us
    all_gather x1, waiting for transfers between devices, shards(): rho_slab = lax.all_gather(rho_part, 'row', axis=1, tiled=True)  152 us
    all_gather x1, waiting for transfers between devices, shards(): own_rows = lax.all_gather(own_slice, 'col', axis=1, tiled=True)  90.3 us
    reduce_scatter x1, waiting for transfers between devices, apply_density(): lax.psum_scatter(cross(rho_slab, basis_block), ('col', 'layer'), scatter_...  69.6 us
    psum x1, waiting for transfers between devices, orthonormalize(): gram_matrix = lax.psum(cross(current, current), ('col', 'layer'))  56.3 us
  transfers between devices with their start and end apart: 12, of which 12 were waited for; matrix products, arithmetic and copies ran while one was open for 0% of the time, Pallas kernels for 0%

commit v1 on v0

--- a/solution.py
+++ b/solution.py
@@ -3,11 +3,18 @@
 import jax.numpy as jnp
 from jax import lax
 from jax.sharding import PartitionSpec as P
+from jax.lax import all_gather
+
+
+def handle_the_plane(x_part, axis_tag):
+    r2 = all_gather(x_part, axis_tag)
+    e_next = jnp.sum(r2, axis=0)
+    return e_next
 
 
 def spread(x, axis, root):
     mine = lax.axis_index(axis) == root
-    return lax.psum(jnp.where(mine, x, jnp.zeros_like(x)), axis)
+    return handle_the_plane(jnp.where(mine, x, jnp.zeros_like(x)), axis_tag=axis)
 
 
 def cross(left, right):

time: 1730 us -> 2100 us (1.21)
  waiting for transfers between devices: 998 us -> 1350 us
    all_gather x0 -> x4, waiting for transfers between devices: none -> 793 us  [handle_the_plane(): r2 = all_gather(x_part, axis_tag)]
    psum x4 -> x0, waiting for transfers between devices: 436 us -> none  [spread(): return lax.psum(jnp.where(mine, x, jnp.zeros_like(x)), axis)]
    reduce_sum x0 -> x4, other arithmetic: none -> 30 us  [handle_the_plane(): e_next = jnp.sum(r2, axis=0)]
where the time goes in v1:
time: 2100 us; the launch traced here: 2090 us
  waiting for transfers between devices  1350 us (64%)
  other arithmetic  520 us (25%)
  matrix products  126 us (6%)
  local copies, waits for them, and re-layouts  65.6 us (3%)
  between operations  24.8 us (1%)
    all_gather x4, waiting for transfers between devices, handle_the_plane(): r2 = all_gather(x_part, axis_tag)  793 us
    another operation x59, other arithmetic, orthonormalize(): factor = jnp.linalg.cholesky(gram_matrix)  317 us
    psum x3, waiting for transfers between devices, orthonormalize(): lax.psum((cross(chosen, current), cross(current, current)), ('col', 'laye...  181 us
    another operation x9, other arithmetic, orthonormalize(): jax.scipy.linalg.solve_triangular(factor, current.T, lower=True)  159 us
    all_gather x1, waiting for transfers between devices, shards(): rho_slab = lax.all_gather(rho_part, 'row', axis=1, tiled=True)  152 us
    all_gather x1, waiting for transfers between devices, shards(): own_rows = lax.all_gather(own_slice, 'col', axis=1, tiled=True)  90.3 us
    reduce_scatter x1, waiting for transfers between devices, apply_density(): lax.psum_scatter(cross(rho_slab, basis_block), ('col', 'layer'), scatter_...  69.6 us
    psum x1, waiting for transfers between devices, orthonormalize(): gram_matrix = lax.psum(cross(current, current), ('col', 'layer'))  56.8 us
  transfers between devices with their start and end apart: 12, of which 12 were waited for; matrix products, arithmetic and copies ran while one was open for 0% of the time, Pallas kernels for 0%

profile of v1, /device:TPU:0, one launch (start us, length us, event | category | flops | bytes accessed | tf_op | source)
XLA Modules:
  0.0 2090.6 jit_solution(3396753527094381356)
XLA Ops:
  9.8 90.3 %all-gather.11.cloned.1.call-done = f32[1024,2048]{1,0:T(8,128)} async-done(((f32[1024,512]{1,0:T(8,128)}), f32[1024,2048]{1,0:T(8,128)}) %all-gather.11.cloned.1.call-update) | async-done | bytes 8388624 | tf_op jit(solution)/shard_map/all_gather | solution.py:66
  108.4 561.5 %all-gather.15.cloned.1.call-done = f32[4096,2048]{1,0:T(8,128)} async-done(((f32[1024,2048]{1,0:T(8,128)}), f32[4096,2048]{1,0:T(8,128)}) %all-gather.15.cloned.1.call-update) | async-done | bytes 33554448 | tf_op jit(solution)/shard_map/all_gather | solution.py:10
  669.9 15.9 reduce_sum.36
  685.8 32.1 %fusion.156 = f32[1024,1024]{1,0:T(8,128)} fusion(f32[1024,2048]{1,0:T(8,128)} %reduce_sum.36, f32[1024,2048]{1,0:T(8,128)} %all-gather.11.cloned.1.call-done), kind=kOutput, calls=%fused_computation.284 | convolution fusion | flops 25769803776 | bytes 20971520 | tf_op jit(solution)/shard_map/dot_general | solution.py:69
  718.0 10.3 reduce-scatter.3.cloned.1.call-done
  728.6 152.1 %all-gather.13.cloned.1.call-done = f32[512,4096]{1,0:T(8,128)} async-done(((f32[512,1024]{1,0:T(8,128)}), f32[512,4096]{1,0:T(8,128)}) %all-gather.13.cloned.1.call-update) | async-done | bytes 8388624 | tf_op jit(solution)/shard_map/all_gather | solution.py:80
  880.7 17.1 fusion.157
  897.8 69.6 %reduce-scatter.5.cloned.1.call-done = f32[512,512]{0,1:T(8,128)} async-done(((f32[4096,512]{0,1:T(8,128)}), f32[512,512]{0,1:T(8,128)}) %reduce-scatter.5.cloned.1.call-update) | async-done | bytes 1048592 | tf_op jit(solution)/shard_map/reduce_scatter | solution.py:35
  972.0 56.8 %all-reduce.9.cloned.1.call-done = f32[512,512]{0,1:T(8,128)} async-done(((f32[512,512]{0,1:T(8,128)}), f32[512,512]{0,1:T(8,128)}) %all-reduce.9.cloned.1.call-update) | async-done | bytes 1048592 | tf_op jit(solution)/shard_map/psum | solution.py:44
  1031.9 11.7 cholesky.462
  1043.6 9.8 custom-call.35
  1054.2 11.7 cholesky.481
  1066.0 10.2 custom-call.36
  1076.8 11.7 cholesky.502
  1089.3 9.8 custom-call.37
  1099.7 11.7 cholesky.519
  1124.1 39.3 %custom-call.38 = f32[4,128,128]{1,2,0:T(8,128)S(1)} custom-call(f32[4,128,128]{2,1,0:T(8,128)S(1)} %get-tuple-element.33), custom_call_target="InvertDiagBlocksLowerTriangular" | custom-call | tf_op jit(solution)/shard_map/jit(_solve_triangular)/triangular_solve | solution.py:47
  1170.8 77.2 %all-gather.17.cloned.1.call-done = f32[2048,512]{0,1:T(8,128)} async-done(((f32[512,512]{0,1:T(8,128)}), f32[2048,512]{0,1:T(8,128)}) %all-gather.17.cloned.1.call-update) | async-done | bytes 4194320 | tf_op jit(solution)/shard_map/all_gather | solution.py:10
  1262.0 60.0 %all-reduce.15.cloned.1.call-done = (f32[512,512]{1,0:T(8,128)}, f32[512,512]{0,1:T(8,128)}) async-done(((f32[512,512]{1,0:T(8,128)}, f32[512,512]{0,1:T(8,128)}), (f32[512,512]{1,0:T(8,128)}, f32[512,512]{0,1:T(8,128)})) %all-reduce.15.cloned.1.call-update) | async-done | bytes 2097168 | tf_op jit(solution)/shard_map/psum | solution.py:52
  1330.5 11.7 cholesky.534
  1342.4 9.8 custom-call.39
  1354.7 11.9 cholesky.553
  1367.9 9.8 custom-call.40
  1379.3 11.7 cholesky.574
  1391.7 9.8 custom-call.41
  1403.4 11.7 cholesky.591
  1427.0 39.3 %custom-call.42 = f32[4,128,128]{1,2,0:T(8,128)S(1)} custom-call(f32[4,128,128]{2,1,0:T(8,128)S(1)} %get-tuple-element.34), custom_call_target="InvertDiagBlocksLowerTriangular" | custom-call | tf_op jit(solution)/shard_map/jit(_solve_triangular)/triangular_solve | solution.py:47
  1473.7 77.0 %all-gather.19.cloned.1.call-done = f32[2048,512]{0,1:T(8,128)} async-done(((f32[512,512]{0,1:T(8,128)}), f32[2048,512]{0,1:T(8,128)}) %all-gather.19.cloned.1.call-update) | async-done | bytes 4194320 | tf_op jit(solution)/shard_map/all_gather | solution.py:10
  1564.4 60.2 %all-reduce.13.cloned.1.call-done = (f32[512,512]{1,0:T(8,128)}, f32[512,512]{0,1:T(8,128)}) async-done(((f32[512,512]{1,0:T(8,128)}, f32[512,512]{0,1:T(8,128)}), (f32[512,512]{1,0:T(8,128)}, f32[512,512]{0,1:T(8,128)})) %all-reduce.13.cloned.1.call-update) | async-done | bytes 2097168 | tf_op jit(solution)/shard_map/psum | solution.py:52
  1633.1 11.7 cholesky.606
  1645.0 9.8 custom-call.43
  1657.3 11.9 cholesky.625
  1670.6 9.8 custom-call.44
  1682.0 11.7 cholesky.646
  1694.4 9.8 custom-call.45
  1706.0 11.7 cholesky.663
  1729.6 39.3 %custom-call.46 = f32[4,128,128]{1,2,0:T(8,128)S(1)} custom-call(f32[4,128,128]{2,1,0:T(8,128)S(1)} %get-tuple-element.35), custom_call_target="InvertDiagBlocksLowerTriangular" | custom-call | tf_op jit(solution)/shard_map/jit(_solve_triangular)/triangular_solve | solution.py:47
  1776.3 77.0 %all-gather.21.cloned.1.call-done = f32[2048,512]{0,1:T(8,128)} async-done(((f32[512,512]{0,1:T(8,128)}), f32[2048,512]{0,1:T(8,128)}) %all-gather.21.cloned.1.call-update) | async-done | bytes 4194320 | tf_op jit(solution)/shard_map/all_gather | solution.py:10
  1867.0 60.5 %all-reduce.11.cloned.1.call-done = (f32[512,512]{1,0:T(8,128)}, f32[512,512]{0,1:T(8,128)}) async-done(((f32[512,512]{1,0:T(8,128)}, f32[512,512]{0,1:T(8,128)}), (f32[512,512]{1,0:T(8,128)}, f32[512,512]{0,1:T(8,128)})) %all-reduce.11.cloned.1.call-update) | async-done | bytes 2097168 | tf_op jit(solution)/shard_map/psum | solution.py:52
  1935.9 11.9 cholesky.678
  1948.0 9.8 custom-call.47
  1960.4 11.7 cholesky.697
  1973.5 9.8 custom-call.48
  1984.9 12.1 cholesky.718
  1997.7 9.8 custom-call.49
  2008.9 11.7 cholesky.735
  2025.0 11.7 while.11
  2036.7 39.5 %custom-call.50 = f32[4,128,128]{1,2,0:T(8,128)S(1)} custom-call(f32[4,128,128]{2,1,0:T(8,128)S(1)} %get-tuple-element.36), custom_call_target="InvertDiagBlocksLowerTriangular" | custom-call | tf_op jit(solution)/shard_map/jit(_solve_triangular)/triangular_solve | solution.py:47
  (230 shorter events, 209.5 us)
Async XLA Ops:
  6.5 874.1 %copy-start = (f32[512,512]{1,0:T(8,128)S(1)}, f32[512,512]{1,0:T(8,128)}, u32[]{:S(2)}) copy-start(f32[512,512]{1,0:T(8,128)} %param.6) | copy-start | bytes 3145732
  6.5 93.6 %all-gather.11.cloned.1.call-start = ((), (), s32[]{:S(2)}) async-start(), calls=%async_computation.2 | async-start | bytes 10485760 | tf_op jit(solution)/shard_map/all_gather | solution.py:66
  9.8 660.1 %all-gather.15.cloned.1.call-start = ((), (), s32[]{:S(2)}) async-start(), calls=%async_computation.7 | async-start | bytes 41943040 | tf_op jit(solution)/shard_map/all_gather | solution.py:10
  108.3 620.0 %reduce-scatter.3.cloned.1.call-start = ((), (), s32[]{:S(2)}) async-start(), calls=%async_computation.3 | async-start | bytes 6291456 | tf_op jit(solution)/shard_map/reduce_scatter | solution.py:68
  717.9 162.7 %all-gather.13.cloned.1.call-start = ((), (), s32[]{:S(2)}) async-start(), calls=%async_computation.4 | async-start | bytes 10485760 | tf_op jit(solution)/shard_map/all_gather | solution.py:80
  728.3 239.1 %reduce-scatter.5.cloned.1.call-start = ((), (), s32[]{:S(2)}) async-start(), calls=%async_computation.5 | async-start | bytes 9437184 | tf_op jit(solution)/shard_map/reduce_scatter | solution.py:35
  897.8 131.0 %all-reduce.9.cloned.1.call-start = ((), (), s32[]{:S(2)}) async-start(), calls=%async_computation.6 | async-start | bytes 2097152 | tf_op jit(solution)/shard_map/psum | solution.py:44
  967.5 196.0 %copy-start.2 = (f32[512,512]{0,1:T(8,128)S(1)}, f32[512,512]{0,1:T(8,128)}, u32[]{:S(2)}) copy-start(f32[512,512]{0,1:T(8,128)} %reduce-scatter.5.cloned.1.call-done) | copy-start | bytes 3145732
  972.0 276.0 %all-gather.17.cloned.1.call-start = ((), (), s32[]{:S(2)}) async-start(), calls=%async_computation.8 | async-start | bytes 5242880 | tf_op jit(solution)/shard_map/all_gather | solution.py:10
  1167.9 154.2 %all-reduce.15.cloned.1.call-start = ((), (), s32[]{:S(2)}) async-start(), calls=%async_computation.13 | async-start | bytes 4194304 | tf_op jit(solution)/shard_map/psum | solution.py:52
  1261.6 289.1 %all-gather.19.cloned.1.call-start = ((), (), s32[]{:S(2)}) async-start(), calls=%async_computation.9 | async-start | bytes 5242880 | tf_op jit(solution)/shard_map/all_gather | solution.py:10
  1329.5 1.0 copy-start.3
  1470.7 154.0 %all-reduce.13.cloned.1.call-start = ((), (), s32[]{:S(2)}) async-start(), calls=%async_computation.12 | async-start | bytes 4194304 | tf_op jit(solution)/shard_map/psum | solution.py:52
  1564.2 289.1 %all-gather.21.cloned.1.call-start = ((), (), s32[]{:S(2)}) async-start(), calls=%async_computation.10 | async-start | bytes 5242880 | tf_op jit(solution)/shard_map/all_gather | solution.py:10
  1632.1 1.0 copy-start.4
  1773.3 154.1 %all-reduce.11.cloned.1.call-start = ((), (), s32[]{:S(2)}) async-start(), calls=%async_computation.11 | async-start | bytes 4194304 | tf_op jit(solution)/shard_map/psum | solution.py:52
  1934.9 1.0 copy-start.5
  1959.0 124.6 %copy-start.1 = (f32[512,512]{1,0:T(8,128)S(1)}, f32[512,512]{1,0:T(8,128)}, u32[]{:S(2)}) copy-start(f32[512,512]{1,0:T(8,128)} %param.6) | copy-start | bytes 3145732
Sparse Core Ops, SparseCore 0:
  9.9 90.1 all-gather.10
  108.5 561.3 all-gather.14
  718.1 10.2 reduce-scatter.2
  729.7 150.8 all-gather.12
  897.9 69.5 reduce-scatter.4
  972.1 56.7 all-reduce.8
  1168.0 79.9 all-gather.16
  1261.7 60.3 all-reduce.14
  1470.8 79.7 all-gather.18
  1564.3 60.3 all-reduce.12
  1773.5 79.7 all-gather.20
  1867.1 60.2 all-reduce.10
